TPU v7x, 32 devices: a whole 2x2x4 slice. The times are simulated.
32 devices in a mesh: row: 4 (over y, x), col: 8 (over z, core).
Axes of the slice: x: 2, y: 2, z: 4, core: 2. Of those that a mesh axis runs over, the one named last changes fastest.
Arguments:
- out_grad: bfloat16 [4096, 512], P('col', 'row'), may hold values from -6 to 6
- node_in: bfloat16 [4096, 512], P(('row', 'col')), may hold values from -0.09375 to 0.09375
- weights: bfloat16 [3, 512, 512], replicated, may hold values from -0.25 to 0.25
- tile_vals: bfloat16 [3, 8, 4, 32, 128, 128], P(None, 'col', 'row'), may hold values from -0.15625 to 0.15625
- tile_rows: int32 [3, 8, 4, 32], P(None, 'col', 'row'), may hold values from 0 to 3
- tile_cols: int32 [3, 8, 4, 32], P(None, 'col', 'row'), may hold values from 0 to 7
- tile_count: int32 [3, 8, 4], P(None, 'col', 'row'), may hold values from 1 to 32, as said below
Outputs:
- d_nodes: bfloat16 [4096, 512], P(('row', 'col'))
- d_weights: float32 [3, 512, 512], replicated
Inputs may be any that keep to these rules, and one draw needn't show every extreme that they name: Only the first tile_count slots of a block's list hold tiles; later slots are ignored. In every relation some block uses all 32 slots. `tile_rows`: coordinates may repeat within a block's list; such tiles add.
All inputs are finite; a program needn't handle non-finite values.
Results may differ from a plain program's by a relative error of at most 0.005.
Values may be sent and summed in bfloat16 or wider, within the bound.
A program may use at most 256 MiB of HBM per device.

v0:
```python
import jax
import jax.numpy as jnp
from jax import lax
from jax.sharding import PartitionSpec as P

group_width = 8


def weight_terms(inputs, sums):
    high_part = sums.astype(jnp.bfloat16)
    low_part = (sums - high_part.astype(jnp.float32)).astype(jnp.bfloat16)
    first = jnp.einsum("nd,rne->rde", inputs, high_part, preferred_element_type=jnp.float32)
    second = jnp.einsum("nd,rne->rde", inputs, low_part, preferred_element_type=jnp.float32)
    return first + second


def tile_sums(tile_block, row_ids, col_ids, count_now, operand, relation, initial, relations):
    tile_size = tile_block.shape[-1]
    feature_width = operand.shape[1] // 2

    def group_step(group_index, partial_stack):
        first_slot = group_index * group_width
        for offset in range(group_width):
            slot_index = first_slot + offset
            values = lax.dynamic_index_in_dim(tile_block, slot_index, 0, keepdims=False)
            source = lax.dynamic_slice_in_dim(
                operand, row_ids[slot_index] * tile_size, tile_size, 0
            )
            product = lax.dot_general(
                values, source, (((0,), (0,)), ((), ())), preferred_element_type=jnp.float32
            )
            product = jnp.where(slot_index < count_now, product, 0.0)
            target = col_ids[slot_index] * tile_size
            own_part = lax.dynamic_slice(
                partial_stack, (relation, target, 0), (1, tile_size, feature_width)
            )
            partial_stack = lax.dynamic_update_slice(
                partial_stack, own_part + product[None, :, :feature_width], (relation, target, 0)
            )
            mixed_part = lax.dynamic_slice(
                partial_stack, (relations, target, 0), (1, tile_size, feature_width)
            )
            partial_stack = lax.dynamic_update_slice(
                partial_stack, mixed_part + product[None, :, feature_width:], (relations, target, 0)
            )
        return partial_stack

    group_count = (count_now + group_width - 1) // group_width
    return lax.fori_loop(0, group_count, group_step, initial)


def body(out_grad, node_in, weights, tile_vals, tile_rows, tile_cols, tile_count):
    grad_block = lax.all_gather(out_grad, "row", axis=1, tiled=True)
    relations = weights.shape[0]
    feature_width = weights.shape[1]
    source_rows = node_in.shape[0] * lax.axis_size("col")
    partial_stack = jnp.zeros((relations + 1, source_rows, feature_width), jnp.float32)
    for relation in range(relations):
        premixed = lax.dot_general(
            grad_block,
            weights[relation],
            (((1,), (1,)), ((), ())),
            preferred_element_type=jnp.float32,
        ).astype(jnp.bfloat16)
        operand = jnp.concatenate([grad_block, premixed], axis=1)
        partial_stack = tile_sums(
            tile_vals[relation, 0, 0],
            tile_rows[relation, 0, 0],
            tile_cols[relation, 0, 0],
            tile_count[relation, 0, 0],
            operand,
            relation,
            partial_stack,
            relations,
        )
    reduced = lax.psum_scatter(partial_stack[relations], "col", scatter_dimension=0, tiled=True)
    d_nodes = reduced.astype(jnp.bfloat16)
    piece = lax.all_gather(node_in, "col", axis=0, tiled=True)
    sums_here = lax.dynamic_slice(
        partial_stack, (0, 0, 0), (relations, piece.shape[0], feature_width)
    )
    local_grads = weight_terms(piece, sums_here)
    d_weights = lax.psum(local_grads, ("row", "col"))
    return (d_nodes, d_weights)


def solution(mesh):
    return jax.shard_map(
        body,
        mesh=mesh,
        in_specs=(
            P("col", "row"),
            P(("row", "col"), None),
            P(),
            P(None, "col", "row", None, None, None),
            P(None, "col", "row", None),
            P(None, "col", "row", None),
            P(None, "col", "row"),
        ),
        out_specs=(P(("row", "col"), None), P()),
        check_vma=False,
    )
```

profile of v0, /device:TPU:0, one launch (start us, length us, event | category | flops | bytes accessed | tf_op | source)
XLA Modules:
  0.0 781.8 jit_solution(16126669114292662267)
XLA Ops:
  10.9 11.5 %all_gather.6 = bf16[512,512]{0,1:T(8,128)(2,1)S(1)} all-gather(bf16[512,128]{0,1:T(8,128)(2,1)S(1)} %copy.9), channel_id=1, replica_groups=mesh['row'=4,'col'=8] {'row'}, dimensions={1}, use_global_device_ids=true | all-gather | bytes 655360 | tf_op jit(solution)/shard_map/all_gather | solution.py:53
  30.3 3.6 slice_bitcast_fusion.49
  34.0 4.3 broadcast_in_dim.331
  38.3 50.7 %while.36 = (s32[]{:T(128)}, f32[4,1024,512]{2,1,0:T(8,128)}, s32[]{:T(128)}, s32[32]{0:T(128)S(1)}, s32[]{:T(128)}, /*index=5*/bf16[32,128,128]{2,1,0:T(8,128)(...) while((s32[]{:T(128)}, f32[4,1024,512]{2,1,0:T(8,128)}, ...), condition=%wide.region_1.2_spmd, body=%wide.region_0.1_spmd.sunk | while | flops 270532640 | bytes 19138228 | solution.py:49
  41.9 1.7 fusion.328
  48.1 1.7 fusion.330
  54.4 1.7 fusion.332
  60.6 1.7 fusion.334
  62.4 1.7 fusion.335
  73.2 1.7 fusion.338
  79.4 1.7 fusion.340
  81.1 1.7 fusion.341
  90.5 151.8 %while.37 = (s32[]{:T(128)}, f32[4,1024,512]{2,1,0:T(8,128)}, s32[]{:T(128)}, s32[32]{0:T(128)S(1)}, s32[]{:T(128)}, /*index=5*/bf16[32,128,128]{2,1,0:T(8,128)(...) while((s32[]{:T(128)}, f32[4,1024,512]{2,1,0:T(8,128)}, ...), condition=%wide.region_3.4_spmd, body=%wide.region_2.3_spmd.sunk | while | flops 270532640 | bytes 19138228 | solution.py:49
  94.1 1.7 fusion.361
  100.2 1.7 fusion.363
  101.9 1.7 fusion.364
  106.4 1.7 fusion.365
  112.7 1.7 fusion.367
  126.9 1.7 fusion.372
  133.1 1.7 fusion.374
  137.7 1.7 fusion.375
  139.4 1.7 fusion.376
  144.6 1.7 fusion.361
  146.3 1.7 fusion.362
  152.4 1.7 fusion.364
  156.9 1.7 fusion.365
  158.6 1.7 fusion.366
  163.3 1.7 fusion.367
  165.0 1.7 fusion.368
  175.8 1.7 fusion.371
  177.5 1.7 fusion.372
  182.0 1.7 fusion.373
  183.7 1.7 fusion.374
  188.3 1.7 fusion.375
  190.0 1.7 fusion.376
  195.2 1.7 fusion.361
  196.9 1.7 fusion.362
  201.4 1.7 fusion.363
  203.1 1.7 fusion.364
  207.6 1.7 fusion.365
  213.9 1.7 fusion.367
  220.1 1.7 fusion.369
  226.4 1.7 fusion.371
  228.1 1.7 fusion.372
  240.5 1.7 fusion.376
  243.7 45.3 %while.38 = (s32[]{:T(128)}, f32[4,1024,512]{2,1,0:T(8,128)}, s32[]{:T(128)}, s32[32]{0:T(128)S(1)}, s32[]{:T(128)}, /*index=5*/bf16[32,128,128]{2,1,0:T(8,128)(...) while((s32[]{:T(128)}, f32[4,1024,512]{2,1,0:T(8,128)}, ...), condition=%wide.region_5.6_spmd, body=%wide.region_4.5_spmd.sunk | while | flops 270532640 | bytes 19138228 | solution.py:49
  246.7 1.7 fusion.394
  248.4 1.7 fusion.395
  252.3 1.7 fusion.396
  257.8 1.7 fusion.398
  265.2 1.7 fusion.401
  270.7 1.7 fusion.403
  274.5 1.7 fusion.404
  280.1 1.7 fusion.406
  281.8 1.7 fusion.407
  285.6 1.7 fusion.408
  287.3 1.7 fusion.409
  289.0 8.7 %copy.13 = f32[4,1024,512]{1,2,0:T(8,128)} copy(f32[4,1024,512]{2,1,0:T(8,128)} %get-tuple-element.334) | data formatting | bytes 16777216 | tf_op jit(solution)/shard_map/while | solution.py:49
  297.7 5.0 fusion.193
  303.4 3.5 add_bitcast_fusion
  307.0 3.2 slice_bitcast_fusion.48
  310.2 426.4 %all-reduce.2.cloned.1.call-done = f32[3,512,512]{1,2,0:T(8,128)} async-done(((f32[3,512,512]{1,2,0:T(8,128)}), f32[3,512,512]{1,2,0:T(8,128)}) %all-reduce.2.cloned.1.call-update) | async-done | bytes 3145744 | tf_op jit(solution)/shard_map/psum | solution.py:83
  736.6 3.5 copy.14
  740.1 33.6 %reduce-scatter.2.cloned.1.call-done = f32[128,512]{1,0:T(8,128)} async-done(((f32[1024,512]{1,0:T(8,128)}), f32[128,512]{1,0:T(8,128)}) %reduce-scatter.2.cloned.1.call-update) | async-done | bytes 262160 | tf_op jit(solution)/shard_map/reduce_scatter | solution.py:76
  (100 shorter events, 101.8 us)
Async XLA Ops:
  7.2 290.5 %all-gather.2.cloned.1.call-start = ((), (), s32[]{:S(2)}) async-start(), calls=%async_computation.2 | async-start | bytes 1179648 | tf_op jit(solution)/shard_map/all_gather | solution.py:78
  7.9 728.7 %all-reduce.2.cloned.1.call-start = ((), (), s32[]{:S(2)}) async-start(), calls=%async_computation.3 | async-start | bytes 6291456 | tf_op jit(solution)/shard_map/psum | solution.py:83
  23.9 10.1 %copy-start.1 = (s32[3,1,1,32]{3,2,1,0:T(1,128)S(1)}, s32[3,1,1,32]{3,2,1,0:T(1,128)}, u32[]{:S(2)}) copy-start(s32[3,1,1,32]{3,2,1,0:T(1,128)} %param.17) | copy-start | bytes 1156
  23.9 10.0 %copy-start.2 = (s32[3,1,1,32]{3,2,1,0:T(1,128)S(1)}, s32[3,1,1,32]{3,2,1,0:T(1,128)}, u32[]{:S(2)}) copy-start(s32[3,1,1,32]{3,2,1,0:T(1,128)} %param.18) | copy-start | bytes 1156
  297.7 5.5 copy-start
  297.7 5.7 copy-start.3
  306.9 466.8 %reduce-scatter.2.cloned.1.call-start = ((), (), s32[]{:S(2)}) async-start(), calls=%async_computation.1 | async-start | bytes 2359296 | tf_op jit(solution)/shard_map/reduce_scatter | solution.py:76
Sparse Core Ops, SparseCore 0:
  9.6 24.9 all-gather.1
  307.0 429.4 all-reduce.1
  738.9 34.7 reduce-scatter.1
where the time goes:
time: 794 us; the launch traced here: 782 us
  waiting for transfers between devices  461 us (58%)
  other arithmetic  139 us (18%)
  loops' own time  74.2 us (9%)
  matrix products  47.2 us (6%)
  local copies, waits for them, and re-layouts  33.6 us (4%)
  between operations  15.7 us (2%)
  blocking collectives  11.5 us (1%)
    psum x1, waiting for transfers between devices, body(): d_weights = lax.psum(local_grads, ('row', 'col'))  426 us
    another operation x3, loops' own time, tile_sums(): return lax.fori_loop(0, group_count, group_step, initial)  74.2 us
    dynamic_update_slice x40, other arithmetic, group_step(): lax.dynamic_update_slice(partial_stack, own_part + product[None, :, :feat...  67.9 us
    dynamic_update_slice x40, other arithmetic, group_step(): lax.dynamic_update_slice(partial_stack, mixed_part + product[None, :, fea...  67.8 us
    dot_general x40, matrix products, group_step(): lax.dot_general(values, source, (((0,), (0,)), ((), ())), preferred_eleme...  34.3 us
    reduce_scatter x1, waiting for transfers between devices, body(): lax.psum_scatter(partial_stack[relations], 'col', scatter_dimension=0, ti...  33.6 us
  transfers between devices with their start and end apart: 3, of which 2 were waited for; matrix products, arithmetic and copies ran while one was open for 27% of the time, Pallas kernels for 0%

commit v1 on v0

--- a/solution.py
+++ b/solution.py
@@ -80,7 +80,7 @@
         partial_stack, (0, 0, 0), (relations, piece.shape[0], feature_width)
     )
     local_grads = weight_terms(piece, sums_here)
-    d_weights = lax.psum(local_grads, ("row", "col"))
+    d_weights = lax.psum(lax.psum(local_grads, "col"), "row")
     return (d_nodes, d_weights)
 
 

time: 794 us -> 825 us (1.039)
  waiting for transfers between devices: 461 us -> 491 us
    psum x1 -> x2, waiting for transfers between devices: 426 us -> 452 us  [body(): d_weights = lax.psum(lax.psum(local_grads, 'col'), 'row')]
  transfers between devices with their start and end apart: 3 -> 4, of which waited for: 2 -> 3; matrix products, arithmetic and copies ran while one was open for 27% -> 25% of each run, Pallas kernels for 0% -> 0%
where the time goes in v1:
time: 825 us; the launch traced here: 812 us
  waiting for transfers between devices  491 us (60%)
  other arithmetic  139 us (17%)
  loops' own time  74.2 us (9%)
  matrix products  47.2 us (6%)
  local copies, waits for them, and re-layouts  33.6 us (4%)
  between operations  15.7 us (2%)
  blocking collectives  11.5 us (1%)
    psum x2, waiting for transfers between devices, body(): d_weights = lax.psum(lax.psum(local_grads, 'col'), 'row')  452 us
    another operation x3, loops' own time, tile_sums(): return lax.fori_loop(0, group_count, group_step, initial)  74.2 us
    dynamic_update_slice x40, other arithmetic, group_step(): lax.dynamic_update_slice(partial_stack, own_part + product[None, :, :feat...  67.9 us
    dynamic_update_slice x40, other arithmetic, group_step(): lax.dynamic_update_slice(partial_stack, mixed_part + product[None, :, fea...  67.8 us
    reduce_scatter x1, waiting for transfers between devices, body(): lax.psum_scatter(partial_stack[relations], 'col', scatter_dimension=0, ti...  38.2 us
    dot_general x40, matrix products, group_step(): lax.dot_general(values, source, (((0,), (0,)), ((), ())), preferred_eleme...  34.3 us
  transfers between devices with their start and end apart: 4, of which 3 were waited for; matrix products, arithmetic and copies ran while one was open for 25% of the time, Pallas kernels for 0%

profile of v1, /device:TPU:0, one launch (start us, length us, event | category | flops | bytes accessed | tf_op | source)
XLA Modules:
  0.0 812.1 jit_solution(1025831593036590659)
XLA Ops:
  10.9 11.5 %all_gather.6 = bf16[512,512]{0,1:T(8,128)(2,1)S(1)} all-gather(bf16[512,128]{0,1:T(8,128)(2,1)S(1)} %copy.9), channel_id=1, replica_groups=mesh['row'=4,'col'=8] {'row'}, dimensions={1}, use_global_device_ids=true | all-gather | bytes 655360 | tf_op jit(solution)/shard_map/all_gather | solution.py:53
  30.3 3.6 slice_bitcast_fusion.49
  34.0 4.3 broadcast_in_dim.331
  38.3 50.7 %while.36 = (s32[]{:T(128)}, f32[4,1024,512]{2,1,0:T(8,128)}, s32[]{:T(128)}, s32[32]{0:T(128)S(1)}, s32[]{:T(128)}, /*index=5*/bf16[32,128,128]{2,1,0:T(8,128)(...) while((s32[]{:T(128)}, f32[4,1024,512]{2,1,0:T(8,128)}, ...), condition=%wide.region_1.2_spmd, body=%wide.region_0.1_spmd.sunk | while | flops 270532640 | bytes 19138228 | solution.py:49
  41.9 1.7 fusion.328
  48.1 1.7 fusion.330
  60.6 1.7 fusion.334
  62.4 1.7 fusion.335
  73.2 1.7 fusion.338
  79.4 1.7 fusion.340
  81.1 1.7 fusion.341
  90.5 151.8 %while.37 = (s32[]{:T(128)}, f32[4,1024,512]{2,1,0:T(8,128)}, s32[]{:T(128)}, s32[32]{0:T(128)S(1)}, s32[]{:T(128)}, /*index=5*/bf16[32,128,128]{2,1,0:T(8,128)(...) while((s32[]{:T(128)}, f32[4,1024,512]{2,1,0:T(8,128)}, ...), condition=%wide.region_3.4_spmd, body=%wide.region_2.3_spmd.sunk | while | flops 270532640 | bytes 19138228 | solution.py:49
  94.1 1.7 fusion.361
  100.2 1.7 fusion.363
  101.9 1.7 fusion.364
  106.4 1.7 fusion.365
  112.7 1.7 fusion.367
  126.9 1.7 fusion.372
  133.1 1.7 fusion.374
  137.7 1.7 fusion.375
  139.4 1.7 fusion.376
  144.6 1.7 fusion.361
  146.3 1.7 fusion.362
  152.4 1.7 fusion.364
  156.9 1.7 fusion.365
  158.6 1.7 fusion.366
  163.3 1.7 fusion.367
  165.0 1.7 fusion.368
  175.8 1.7 fusion.371
  177.5 1.7 fusion.372
  182.0 1.7 fusion.373
  183.7 1.7 fusion.374
  188.3 1.7 fusion.375
  190.0 1.7 fusion.376
  195.2 1.7 fusion.361
  196.9 1.7 fusion.362
  201.4 1.7 fusion.363
  203.1 1.7 fusion.364
  207.6 1.7 fusion.365
  213.9 1.7 fusion.367
  220.1 1.7 fusion.369
  226.4 1.7 fusion.371
  228.1 1.7 fusion.372
  240.5 1.7 fusion.376
  243.7 45.3 %while.38 = (s32[]{:T(128)}, f32[4,1024,512]{2,1,0:T(8,128)}, s32[]{:T(128)}, s32[32]{0:T(128)S(1)}, s32[]{:T(128)}, /*index=5*/bf16[32,128,128]{2,1,0:T(8,128)(...) while((s32[]{:T(128)}, f32[4,1024,512]{2,1,0:T(8,128)}, ...), condition=%wide.region_5.6_spmd, body=%wide.region_4.5_spmd.sunk | while | flops 270532640 | bytes 19138228 | solution.py:49
  246.7 1.7 fusion.394
  248.4 1.7 fusion.395
  252.3 1.7 fusion.396
  257.8 1.7 fusion.398
  265.2 1.7 fusion.401
  270.7 1.7 fusion.403
  274.5 1.7 fusion.404
  280.1 1.7 fusion.406
  281.8 1.7 fusion.407
  285.6 1.7 fusion.408
  287.3 1.7 fusion.409
  289.0 8.7 %copy.13 = f32[4,1024,512]{1,2,0:T(8,128)} copy(f32[4,1024,512]{2,1,0:T(8,128)} %get-tuple-element.334) | data formatting | bytes 16777216 | tf_op jit(solution)/shard_map/while | solution.py:49
  297.7 5.0 fusion.193
  303.4 3.5 add_bitcast_fusion
  307.0 3.2 slice_bitcast_fusion.48
  310.3 365.0 %all-reduce.3.cloned.1.call-done = f32[3,512,512]{1,2,0:T(8,128)} async-done(((f32[3,512,512]{1,2,0:T(8,128)}), f32[3,512,512]{1,2,0:T(8,128)}) %all-reduce.3.cloned.1.call-update) | async-done | bytes 3145744 | tf_op jit(solution)/shard_map/psum | solution.py:83
  675.3 38.2 %reduce-scatter.2.cloned.1.call-done = f32[128,512]{1,0:T(8,128)} async-done(((f32[1024,512]{1,0:T(8,128)}), f32[128,512]{1,0:T(8,128)}) %reduce-scatter.2.cloned.1.call-update) | async-done | bytes 262160 | tf_op jit(solution)/shard_map/reduce_scatter | solution.py:76
  715.1 86.9 %all-reduce.5.cloned.1.call-done = f32[3,512,512]{1,2,0:T(8,128)} async-done(((f32[3,512,512]{1,2,0:T(8,128)}), f32[3,512,512]{1,2,0:T(8,128)}) %all-reduce.5.cloned.1.call-update) | async-done | bytes 3145744 | tf_op jit(solution)/shard_map/psum | solution.py:83
  802.0 3.5 copy.14
  (103 shorter events, 103.5 us)
Async XLA Ops:
  7.2 290.5 %all-gather.2.cloned.1.call-start = ((), (), s32[]{:S(2)}) async-start(), calls=%async_computation.2 | async-start | bytes 1179648 | tf_op jit(solution)/shard_map/all_gather | solution.py:78
  7.9 667.4 %all-reduce.3.cloned.1.call-start = ((), (), s32[]{:S(2)}) async-start(), calls=%async_computation.3 | async-start | bytes 6291456 | tf_op jit(solution)/shard_map/psum | solution.py:83
  23.9 10.1 %copy-start.1 = (s32[3,1,1,32]{3,2,1,0:T(1,128)S(1)}, s32[3,1,1,32]{3,2,1,0:T(1,128)}, u32[]{:S(2)}) copy-start(s32[3,1,1,32]{3,2,1,0:T(1,128)} %param.17) | copy-start | bytes 1156
  23.9 10.0 %copy-start.2 = (s32[3,1,1,32]{3,2,1,0:T(1,128)S(1)}, s32[3,1,1,32]{3,2,1,0:T(1,128)}, u32[]{:S(2)}) copy-start(s32[3,1,1,32]{3,2,1,0:T(1,128)} %param.18) | copy-start | bytes 1156
  297.7 5.5 copy-start
  297.7 5.7 copy-start.3
  306.9 406.6 %reduce-scatter.2.cloned.1.call-start = ((), (), s32[]{:S(2)}) async-start(), calls=%async_computation.1 | async-start | bytes 2359296 | tf_op jit(solution)/shard_map/reduce_scatter | solution.py:76
  310.2 491.8 %all-reduce.5.cloned.1.call-start = ((), (), s32[]{:S(2)}) async-start(), calls=%async_computation.4 | async-start | bytes 6291456 | tf_op jit(solution)/shard_map/psum | solution.py:83
Sparse Core Ops, SparseCore 0:
  9.6 24.9 all-gather.1
  307.0 368.1 all-reduce.2
  677.6 35.9 reduce-scatter.1
  716.5 85.5 all-reduce.4
